TPU v7x, 32 devices: a whole 2x2x4 slice. The times are simulated.
32 devices in a mesh: grp: 2 (over x), dev: 16 (over z, y, core).
Axes of the slice: x: 2, y: 2, z: 4, core: 2. Of those that a mesh axis runs over, the one named last changes fastest.
Arguments:
- inputs: bfloat16 [64, 196, 1024], P(('grp', 'dev')), may hold values from -6 to 6
- cotangent: bfloat16 [64, 196, 1024], P(('grp', 'dev')), may hold values from -6 to 6
- first_gain: float32 [1024], replicated, may hold values from 0.5 to 1.5
- first_shift: float32 [1024], replicated, may hold values from -3 to 3
- token_in: bfloat16 [512, 196], replicated, may hold values from -0.4375 to 0.4375
- token_in_bias: float32 [512], replicated, may hold values from -3 to 3
- token_out: bfloat16 [512, 196], replicated, may hold values from -0.25 to 0.25
- second_gain: float32 [1024], replicated, may hold values from 0.5 to 1.5
- second_shift: float32 [1024], replicated, may hold values from -3 to 3
- channel_in: bfloat16 [1024, 4096], replicated, may hold values from -0.1875 to 0.1875
- channel_in_bias: float32 [4096], replicated, may hold values from -3 to 3
- channel_out: bfloat16 [1024, 4096], replicated, may hold values from -0.09375 to 0.09375
Outputs:
- grad_inputs: bfloat16 [64, 196, 1024], P(('grp', 'dev'))
- grad_token_in: float32 [512, 196], P('dev')
- grad_token_out: float32 [512, 196], P('dev')
- grad_channel_in: float32 [1024, 4096], P('dev')
- grad_channel_out: float32 [1024, 4096], P('dev')
- grad_norms: float32 [5, 1024], replicated
- grad_token_in_bias: float32 [512], replicated
- grad_token_out_bias: float32 [196], replicated
- grad_channel_in_bias: float32 [4096], replicated
All inputs are finite; a program needn't handle non-finite values.
Results may differ from a plain program's by a relative error of at most 0.0066.
Values sent between devices are 32-bit elements; how exact they have to be, the bound alone decides.
A program may use at most 192 MiB of HBM per device.

v0:
```python
import math
import jax
import jax.numpy as jnp
from jax import lax
from jax.sharding import PartitionSpec as P

epsilon = 1e-06


def norm_forward(values, gain, shift):
    centred = values - jnp.mean(values, axis=-1, keepdims=True)
    variance = jnp.mean(centred * centred, axis=-1, keepdims=True)
    inv_std = lax.rsqrt(variance + epsilon)
    scaled = centred * inv_std
    return (scaled * gain + shift, scaled, inv_std)


def norm_backward(incoming, scaled, inv_std, gain):
    weighted = incoming * gain
    first_mean = jnp.mean(weighted, axis=-1, keepdims=True)
    second_mean = jnp.mean(weighted * scaled, axis=-1, keepdims=True)
    return inv_std * (weighted - first_mean - scaled * second_mean)


def gelu_value(values):
    return 0.5 * values * (1.0 + lax.erf(values / math.sqrt(2.0)))


def gelu_slope(values):
    return 0.5 * (1.0 + lax.erf(values / math.sqrt(2.0))) + values * jnp.exp(
        -0.5 * values * values
    ) / math.sqrt(2.0 * math.pi)


def per_device(
    inputs,
    cotangent,
    first_gain,
    first_shift,
    token_in,
    token_in_bias,
    token_out,
    second_gain,
    second_shift,
    channel_in,
    channel_in_bias,
    channel_out,
):
    f32 = jnp.float32
    images, patches, channels = inputs.shape
    x_float = inputs.astype(f32)
    g_float = cotangent.astype(f32)
    normed_one, first_hat, first_rstd = norm_forward(x_float, first_gain, first_shift)
    normed1 = normed_one.astype(jnp.bfloat16)
    hidden1 = (
        jnp.einsum("bpc,sp->bcs", normed1, token_in, preferred_element_type=f32) + token_in_bias
    )
    act1 = gelu_value(hidden1).astype(jnp.bfloat16)
    mixed = x_float + jnp.einsum("bcs,sp->bpc", act1, token_out, preferred_element_type=f32)
    normed_two, second_hat, second_rstd = norm_forward(mixed, second_gain, second_shift)
    normed2 = normed_two.astype(jnp.bfloat16).reshape(-1, channels)
    hidden2 = jnp.dot(normed2, channel_in, preferred_element_type=f32) + channel_in_bias
    act2 = gelu_value(hidden2).astype(jnp.bfloat16)
    cot_rows = cotangent.reshape(-1, channels)
    piece = cot_rows
    chout_part = lax.psum_scatter(
        jnp.einsum("tc,tk->ck", piece, act2, preferred_element_type=f32),
        "dev",
        scatter_dimension=0,
        tiled=True,
    )
    dact2 = jnp.dot(cot_rows, channel_out, preferred_element_type=f32)
    dhidden2 = (dact2 * gelu_slope(hidden2)).astype(jnp.bfloat16)
    piece = normed2
    chin_part = lax.psum_scatter(
        jnp.einsum("tc,tk->ck", piece, dhidden2, preferred_element_type=f32),
        "dev",
        scatter_dimension=0,
        tiled=True,
    )
    dnormed2 = jnp.einsum("tk,ck->tc", dhidden2, channel_in, preferred_element_type=f32).reshape(
        images, patches, channels
    )
    dmixed = g_float + norm_backward(dnormed2, second_hat, second_rstd, second_gain)
    dmixed_round = dmixed.astype(jnp.bfloat16)
    dact1 = jnp.einsum("bpc,sp->bcs", dmixed_round, token_out, preferred_element_type=f32)
    dhidden1 = (dact1 * gelu_slope(hidden1)).astype(jnp.bfloat16)
    dnormed1 = jnp.einsum("bcs,sp->bpc", dhidden1, token_in, preferred_element_type=f32)
    grad_inputs = (dmixed + norm_backward(dnormed1, first_hat, first_rstd, first_gain)).astype(
        jnp.bfloat16
    )
    grad_in_piece = jnp.einsum("bcs,bpc->sp", dhidden1, normed1, preferred_element_type=f32)
    grad_out_piece = jnp.einsum("bcs,bpc->sp", act1, dmixed_round, preferred_element_type=f32)
    token_part = lax.psum_scatter(
        jnp.concatenate([grad_in_piece, grad_out_piece], axis=1),
        "dev",
        scatter_dimension=0,
        tiled=True,
    )
    token_part, chin_part, chout_part = lax.psum((token_part, chin_part, chout_part), "grp")
    norms_part = jnp.stack(
        [
            jnp.sum(dnormed1 * first_hat, axis=(0, 1)),
            jnp.sum(dnormed1, axis=(0, 1)),
            jnp.sum(dnormed2 * second_hat, axis=(0, 1)),
            jnp.sum(dnormed2, axis=(0, 1)),
            jnp.sum(g_float, axis=(0, 1)),
        ]
    )
    tb_in = jnp.sum(dhidden1.astype(f32), axis=(0, 1))
    tb_out = jnp.sum(dmixed, axis=(0, 2))
    cb_in = jnp.sum(dhidden2.astype(f32), axis=0)
    norms_total, tb_in_total, tb_out_total, cb_in_total = lax.psum(
        (norms_part, tb_in, tb_out, cb_in), ("grp", "dev")
    )
    return (
        grad_inputs,
        token_part[:, :patches],
        token_part[:, patches:],
        chin_part,
        chout_part,
        norms_total,
        tb_in_total,
        tb_out_total,
        cb_in_total,
    )


def solution(mesh):
    in_specs = (
        P(("grp", "dev"), None, None),
        P(("grp", "dev"), None, None),
        P(),
        P(),
        P(),
        P(),
        P(),
        P(),
        P(),
        P(),
        P(),
        P(),
    )
    out_specs = (
        P(("grp", "dev"), None, None),
        P("dev", None),
        P("dev", None),
        P("dev", None),
        P("dev", None),
        P(),
        P(),
        P(),
        P(),
    )
    return jax.shard_map(
        per_device, mesh=mesh, in_specs=in_specs, out_specs=out_specs, check_vma=False
    )
```

profile of v0, /device:TPU:0, one launch (start us, length us, event | category | flops | bytes accessed | tf_op | source)
XLA Modules:
  0.0 573.7 jit_solution(3581374591141366518)
XLA Ops:
  7.2 1.5 convert_reduce_fusion.2
  8.7 1.5 fusion.28
  10.3 4.7 multiply_convert_fusion.1
  18.5 6.4 %fusion.47 = f32[392,4096]{1,0:T(8,128)S(1)} fusion(bf16[392,1024]{1,0:T(8,128)(2,1)} %reshape.80, bf16[1024,4096]{1,0:T(8,128)(2,1)} %param.21), kind=kOutput, calls=%fused_computation.77 | convolution fusion | flops 3288334336 | bytes 15613952 | tf_op jit(solution)/shard_map/dot_general | solution.py:62
  24.9 2.6 copy-done.21
  27.5 8.2 %convolution_bitcast_fusion = f32[1024,4096]{0,1:T(8,128)} fusion(bf16[392,1024]{1,0:T(8,128)(2,1)S(1)} %reshape.79, f32[392,4096]{1,0:T(8,128)S(1)} %fusion.47, f32[4096]{0:T(1024)S(1)} %copy-done.18), kind=kOutput, calls=%fused_computation.1 | convolution fusion | flops 3297968128 | bytes 24018944 | tf_op jit(solution)/shard_map/tc,tk->ck/dot_general | solution.py:67
  35.7 17.5 %copy.43 = f32[1024,4096]{1,0:T(8,128)} copy(f32[1024,4096]{0,1:T(8,128)} %convolution_bitcast_fusion) | data formatting | bytes 33554432
  54.3 8.6 %convert_reduce_fusion = (f32[4096]{0:T(1024)S(1)}, bf16[392,4096]{1,0:T(8,128)(2,1)S(1)}) fusion(f32[392,4096]{1,0:T(8,128)} %copy-done.21, f32[4096]{0:T(1024)S(1)} %copy-done.18, bf16[392,1024]{1,0:T(8,128)(2,1)S(1)} %copy-done.12, bf16[1024,4096]{1,0:T(8,128)(2,1)} %param.23), kind=kOutput, calls=%fused_computation.8 | convolution fusion | flops 3309203456 | bytes 18857984 | tf_op jit(solution)/shard_map/dot_general | solution.py:72
  62.9 1.8 copy-done.24
  64.8 11.0 %fusion.48 = f32[1024,4096]{1,0:T(8,128)} fusion(bf16[392,1024]{1,0:T(8,128)(2,1)S(1)} %copy-done.10, bf16[392,4096]{1,0:T(8,128)(2,1)S(1)} %get-tuple-element.63), kind=kOutput, calls=%fused_computation.78 | convolution fusion | flops 3288334336 | bytes 20791296 | tf_op jit(solution)/shard_map/tc,tk->ck/dot_general | solution.py:76
  75.8 11.2 %fusion.43 = (f32[1024]{0:T(1024)S(1)}, f32[392]{0:T(512)S(1)}, f32[392,1024]{1,0:T(8,128)}) fusion(f32[1024]{0:T(1024)S(1)} %copy-done.15, bf16[392,4096]{1,0:T(8,128)(2,1)} %copy-done.24, bf16[1024,4096]{1,0:T(8,128)(2,1)} %param.21), kind=kOutput, calls=%fused_computation.73 | convolution fusion | flops 3289537024 | bytes 13215264 | tf_op jit(solution)/shard_map/tk,ck->tc/dot_general | solution.py:81
  87.0 1.6 reshape.81
  92.0 1.3 copy-done.22
  93.5 2.4 convert_reduce_fusion.1
  98.6 134.7 %reduce-scatter.12.cloned.1.call-done = f32[64,4096]{1,0:T(8,128)} async-done(((f32[1024,4096]{1,0:T(8,128)}), f32[64,4096]{1,0:T(8,128)}) %reduce-scatter.12.cloned.1.call-update) | async-done | bytes 1048592
  233.4 3.2 copy.44
  236.6 177.4 %reduce-scatter.8.cloned.1.call-done = f32[64,4096]{1,0:T(8,128)} async-done(((f32[1024,4096]{1,0:T(8,128)}), f32[64,4096]{1,0:T(8,128)}) %reduce-scatter.8.cloned.1.call-update) | async-done | bytes 1048592 | tf_op jit(solution)/shard_map/reduce_scatter | solution.py:75
  414.0 2.8 fusion.27
  417.5 1.7 copy.37
  419.3 40.5 %all-reduce = (f32[5,1024]{1,0:T(8,128)}, f32[512]{0:T(512)}, f32[196]{0:T(256)}, f32[4096]{0:T(1024)}) all-reduce(f32[5,1024]{1,0:T(8,128)S(1)} %stack.23, f32[512]{0:T(512)S(1)} %get-tuple-element.60, f32[196]{0:T(256)S(1)} %get-tuple-element.49, f32[4096]{0:T(1024)S(1)} %get-tuple-element.62), channel_id=1, replica_groups=mesh['grp'=2,'dev'=16] {'grp','dev'}, use_global_device_ids=true, to_apply=%region_19.0 | all-reduce | flops 9924 | bytes 79392 | tf_op jit(solution)/shard_map/psum | solution.py:113
  459.8 15.0 %reduce-scatter.10.cloned.1.call-done = f32[32,392]{1,0:T(8,128)} async-done(((f32[512,392]{1,0:T(8,128)}), f32[32,392]{1,0:T(8,128)}) %reduce-scatter.10.cloned.1.call-update) | async-done | bytes 50192
  475.8 13.4 %psum.49 = f32[32,392]{0,1:T(8,128)S(1)} all-reduce(f32[32,392]{0,1:T(8,128)S(1)} %copy.42), channel_id=1, replica_groups=mesh['grp'=2,'dev'=16] {'grp'}, use_global_device_ids=true, to_apply=%region_9.0 | all-reduce | flops 12544 | bytes 100352 | tf_op jit(solution)/shard_map/psum | solution.py:100
  490.6 72.4 %all-reduce.4.cloned.1.call-done = (f32[64,4096]{1,0:T(8,128)}, f32[64,4096]{0,1:T(8,128)}) async-done(((f32[64,4096]{1,0:T(8,128)}, f32[64,4096]{0,1:T(8,128)}), (f32[64,4096]{1,0:T(8,128)}, f32[64,4096]{0,1:T(8,128)})) %all-reduce.4.cloned.1.call-update) | async-done | bytes 2097168 | tf_op jit(solution)/shard_map/psum | solution.py:100
  563.0 3.2 copy.40
  (83 shorter events, 15.0 us)
Async XLA Ops:
  7.2 3.1 copy-start
  7.2 226.2 %reduce-scatter.12.cloned.1.call-start = ((), (), s32[]{:S(2)}) async-start(), calls=%async_computation.5 | async-start | bytes 17825792
  10.3 4.7 copy-start.3
  10.3 4.7 copy-start.13
  15.0 1.6 copy-start.15
  15.0 1.6 copy-start.16
  18.4 6.4 %copy-start.11 = (bf16[392,1024]{1,0:T(8,128)(2,1)}, bf16[392,1024]{1,0:T(8,128)(2,1)S(1)}, u32[]{:S(2)}) copy-start(bf16[392,1024]{1,0:T(8,128)(2,1)S(1)} %reshape.79) | copy-start | bytes 2408452
  18.4 9.1 %copy-start.18 = (f32[4096]{0:T(1024)S(1)}, f32[4096]{0:T(1024)}, u32[]{:S(2)}) copy-start(f32[4096]{0:T(1024)} %param.22) | copy-start | bytes 49156
  24.9 2.6 copy-start.21
  53.2 11.6 %copy-start.10 = (bf16[392,1024]{1,0:T(8,128)(2,1)S(1)}, bf16[392,1024]{1,0:T(8,128)(2,1)}, u32[]{:S(2)}) copy-start(bf16[392,1024]{1,0:T(8,128)(2,1)} %reshape.80) | copy-start | bytes 2408452
  53.2 360.8 %reduce-scatter.8.cloned.1.call-start = ((), (), s32[]{:S(2)}) async-start(), calls=%async_computation.3 | async-start | bytes 17825792 | tf_op jit(solution)/shard_map/reduce_scatter | solution.py:75
  62.9 1.8 copy-start.24
  75.8 399.1 %reduce-scatter.10.cloned.1.call-start = ((), (), s32[]{:S(2)}) async-start(), calls=%async_computation.4 | async-start | bytes 1114112
  89.8 1.6 copy-start.6
  89.8 3.5 copy-start.22
  90.7 5.1 copy-start.1
  90.7 2.7 copy-start.14
  90.8 2.7 copy-start.20
  93.5 2.4 copy-start.4
  93.5 2.4 copy-start.17
  93.5 2.4 copy-start.19
  98.6 464.4 %all-reduce.4.cloned.1.call-start = ((), (), s32[]{:S(2)}) async-start(), calls=%async_computation.6 | async-start | bytes 6291456 | tf_op jit(solution)/shard_map/psum | solution.py:100
  414.0 2.9 copy-start.2
  563.0 3.2 copy-start.9
  (5 other events, 6.3 us)
Sparse Core Ops, SparseCore 0:
  53.3 180.0 reduce-scatter.11
  237.5 176.4 reduce-scatter.7
  418.1 56.6 reduce-scatter.9
  477.0 85.9 all-reduce.3
where the time goes:
time: 574 us
  waiting for transfers between devices  400 us (70%)
  matrix products  57.4 us (10%)
  blocking collectives  53.9 us (9%)
  local copies, waits for them, and re-layouts  42.3 us (7%)
  between operations  14.1 us (2%)
  other arithmetic  6.07 us (1%)
    reduce_scatter x1, waiting for transfers between devices, per_device(): lax.psum_scatter(jnp.einsum('tc,tk->ck', piece, dhidden2, preferred_eleme...  177 us
    unnamed x6, waiting for transfers between devices  150 us
    psum x1, waiting for transfers between devices, per_device(): lax.psum((token_part, chin_part, chout_part), 'grp')  72.4 us
    psum x1, blocking collectives, per_device(): lax.psum((norms_part, tb_in, tb_out, cb_in), ('grp', 'dev'))  40.5 us
    unnamed x60, local copies, waits for them, and re-layouts  39.4 us
    psum x1, blocking collectives, per_device(): lax.psum((token_part, chin_part, chout_part), 'grp')  13.4 us
  transfers between devices with their start and end apart: 4, of which 4 were waited for; matrix products, arithmetic and copies ran while one was open for 9% of the time, Pallas kernels for 0%

commit v1 on v0

--- a/solution.py
+++ b/solution.py
@@ -5,6 +5,10 @@
 from jax.sharding import PartitionSpec as P
 
 epsilon = 1e-06
+
+
+def group_set(point):
+    return lax.psum(lax.psum(point, "dev"), "grp")
 
 
 def norm_forward(values, gain, shift):
@@ -110,8 +114,8 @@
     tb_in = jnp.sum(dhidden1.astype(f32), axis=(0, 1))
     tb_out = jnp.sum(dmixed, axis=(0, 2))
     cb_in = jnp.sum(dhidden2.astype(f32), axis=0)
-    norms_total, tb_in_total, tb_out_total, cb_in_total = lax.psum(
-        (norms_part, tb_in, tb_out, cb_in), ("grp", "dev")
+    norms_total, tb_in_total, tb_out_total, cb_in_total = group_set(
+        (norms_part, tb_in, tb_out, cb_in)
     )
     return (
         grad_inputs,

time: 574 us -> 601 us (1.047)
  waiting for transfers between devices: 400 us -> 419 us
  blocking collectives: 53.9 us -> 63.8 us
    psum x1 -> x2, waiting for transfers between devices: 72.4 us -> 108 us  [per_device(): lax.psum((token_part, chin_part, chout_part), 'grp')]
    unnamed x6 -> x7, waiting for transfers between devices: 150 us -> 133 us
    psum x2 -> x1, blocking collectives: 53.9 us -> 63.8 us  [group_set(): return lax.psum(lax.psum(point, 'dev'), 'grp')]
    dot_general x1, matrix products: 11.2 us -> 4.76 us  [per_device(): jnp.einsum('tk,ck->tc', dhidden2, channel_in, preferred_element_type=f32)]
    unnamed x60 -> x78, local copies, waits for them, and re-layouts: 39.4 us -> 36.5 us
  transfers between devices with their start and end apart: 4 -> 5, of which waited for: 4 -> 4; matrix products, arithmetic and copies ran while one was open for 9% -> 9% of each run, Pallas kernels for 0% -> 0%
where the time goes in v1:
time: 601 us; the launch traced here: 600 us
  waiting for transfers between devices  419 us (70%)
  blocking collectives  63.8 us (11%)
  matrix products  53.9 us (9%)
  local copies, waits for them, and re-layouts  40.4 us (7%)
  between operations  14.2 us (2%)
  other arithmetic  8.77 us (1%)
    reduce_scatter x1, waiting for transfers between devices, per_device(): lax.psum_scatter(jnp.einsum('tc,tk->ck', piece, dhidden2, preferred_eleme...  177 us
    unnamed x7, waiting for transfers between devices  133 us
    psum x2, waiting for transfers between devices, per_device(): lax.psum((token_part, chin_part, chout_part), 'grp')  108 us
    psum x1, blocking collectives, group_set(): return lax.psum(lax.psum(point, 'dev'), 'grp')  63.8 us
    unnamed x78, local copies, waits for them, and re-layouts  36.5 us
  transfers between devices with their start and end apart: 5, of which 4 were waited for; matrix products, arithmetic and copies ran while one was open for 9% of the time, Pallas kernels for 0%

profile of v1, /device:TPU:0, one launch (start us, length us, event | category | flops | bytes accessed | tf_op | source)
XLA Modules:
  0.0 599.9 jit_solution(5412226969463608286)
XLA Ops:
  7.2 1.5 convert_reduce_fusion.2
  8.7 1.5 fusion.28
  10.3 4.6 multiply_convert_fusion.1
  18.4 6.7 %fusion.47 = f32[392,4096]{1,0:T(8,128)S(1)} fusion(bf16[392,1024]{1,0:T(8,128)(2,1)} %reshape.80, bf16[1024,4096]{1,0:T(8,128)(2,1)} %param.21), kind=kOutput, calls=%fused_computation.77 | convolution fusion | flops 3288334336 | bytes 15613952 | tf_op jit(solution)/shard_map/dot_general | solution.py:66
  25.2 10.0 %convert_reduce_fusion = (f32[4096]{0:T(1024)S(1)}, bf16[392,4096]{1,0:T(8,128)(2,1)S(1)}) fusion(f32[392,4096]{1,0:T(8,128)S(1)} %fusion.47, f32[4096]{0:T(1024)S(1)} %copy-done.22, bf16[392,1024]{1,0:T(8,128)(2,1)S(1)} %reshape.79, bf16[1024,4096]{1,0:T(8,128)(2,1)} %param.23), kind=kOutput, calls=%fused_computation.8 | convolution fusion | flops 3309203456 | bytes 18857984 | tf_op jit(solution)/shard_map/dot_general | solution.py:76
  35.2 4.8 fusion.43
  40.0 1.6 reshape.81
  42.3 2.2 fusion.44
  45.8 2.4 convert_reduce_fusion.1
  49.6 1.3 copy.41
  51.0 10.4 %convolution_bitcast_fusion = f32[1024,4096]{0,1:T(8,128)} fusion(bf16[392,1024]{1,0:T(8,128)(2,1)S(1)} %copy-done.12, f32[392,4096]{1,0:T(8,128)} %copy-done.26, f32[4096]{0:T(1024)S(1)} %copy-done.23), kind=kOutput, calls=%fused_computation.1 | convolution fusion | flops 3297968128 | bytes 24018944 | tf_op jit(solution)/shard_map/tc,tk->ck/dot_general | solution.py:71
  61.5 17.6 %copy.43 = f32[1024,4096]{1,0:T(8,128)} copy(f32[1024,4096]{0,1:T(8,128)} %convolution_bitcast_fusion) | data formatting | bytes 33554432
  80.2 10.1 %fusion.48 = f32[1024,4096]{1,0:T(8,128)} fusion(bf16[392,1024]{1,0:T(8,128)(2,1)S(1)} %copy-done.10, bf16[392,4096]{1,0:T(8,128)(2,1)} %copy-done.29), kind=kOutput, calls=%fused_computation.78 | convolution fusion | flops 3288334336 | bytes 20791296 | tf_op jit(solution)/shard_map/tc,tk->ck/dot_general | solution.py:80
  90.4 2.7 fusion.27
  93.3 63.8 %all-reduce = (f32[5,1024]{1,0:T(8,128)}, f32[512]{0:T(512)}, f32[196]{0:T(256)}, f32[4096]{0:T(1024)}) all-reduce(f32[5,1024]{1,0:T(8,128)S(1)} %stack.23, f32[512]{0:T(512)S(1)} %get-tuple-element.65, f32[196]{0:T(256)S(1)} %get-tuple-element.54, f32[4096]{0:T(1024)S(1)} %get-tuple-element.67), channel_id=1, replica_groups=mesh['grp'=2,'dev'=16] {'dev'}, use_global_device_ids=true, to_apply=%region_19.0 | all-reduce | flops 9924 | bytes 79392 | tf_op jit(solution)/shard_map/psum | solution.py:11
  157.1 1.7 copy.42
  158.9 133.1 %reduce-scatter.12.cloned.1.call-done = f32[64,4096]{1,0:T(8,128)} async-done(((f32[1024,4096]{1,0:T(8,128)}), f32[64,4096]{1,0:T(8,128)}) %reduce-scatter.12.cloned.1.call-update) | async-done | bytes 1048592
  292.0 3.2 copy.44
  295.2 177.4 %reduce-scatter.8.cloned.1.call-done = f32[64,4096]{1,0:T(8,128)} async-done(((f32[1024,4096]{1,0:T(8,128)}), f32[64,4096]{1,0:T(8,128)}) %reduce-scatter.8.cloned.1.call-update) | async-done | bytes 1048592 | tf_op jit(solution)/shard_map/reduce_scatter | solution.py:79
  472.6 2.0 fusion.26
  474.6 1.7 copy.37
  476.3 22.3 %all-reduce.6.cloned.1.call-done = (f32[32,392]{0,1:T(8,128)}, f32[5,1024]{1,0:T(8,128)}, f32[512]{0:T(512)}, f32[196]{0:T(256)}, f32[4096]{0:T(1024)}) async-done(((f32[32,392]{0,1:T(8,128)}, f32[5,1024]{1,0:T(8,128)}, f32[512]{0:T(512)}, f32[196]{0:T(256)}, f32[4096]{0:T(1024)}), (f32[32,392]{0,1:T(8,128)}, f32[5,1024]{1,0:T(8,128)}, f32[512]{0:T(512)}, f32[196]{0:T(256)}, ...) | async-done | bytes 89888 | tf_op jit(solution)/shard_map/psum | solution.py:104
  501.0 85.8 %all-reduce.8.cloned.1.call-done = (f32[64,4096]{1,0:T(8,128)}, f32[64,4096]{0,1:T(8,128)}) async-done(((f32[64,4096]{1,0:T(8,128)}, f32[64,4096]{0,1:T(8,128)}), (f32[64,4096]{1,0:T(8,128)}, f32[64,4096]{0,1:T(8,128)})) %all-reduce.8.cloned.1.call-update) | async-done | bytes 2097168 | tf_op jit(solution)/shard_map/psum | solution.py:104
  586.8 3.2 copy.40
  (104 shorter events, 14.1 us)
Async XLA Ops:
  7.2 3.1 copy-start
  7.2 149.9 %reduce-scatter.10.cloned.1.call-start = ((), (), s32[]{:S(2)}) async-start(), calls=%async_computation.4 | async-start | bytes 1114112
  10.3 4.7 copy-start.3
  10.3 4.7 copy-start.13
  18.4 6.7 %copy-start.11 = (bf16[392,1024]{1,0:T(8,128)(2,1)}, bf16[392,1024]{1,0:T(8,128)(2,1)S(1)}, u32[]{:S(2)}) copy-start(bf16[392,1024]{1,0:T(8,128)(2,1)S(1)} %reshape.79) | copy-start | bytes 2408452
  18.4 6.7 %copy-start.22 = (f32[4096]{0:T(1024)S(1)}, f32[4096]{0:T(1024)}, u32[]{:S(2)}) copy-start(f32[4096]{0:T(1024)} %param.22) | copy-start | bytes 49156
  18.4 16.8 %slice-start = ((s8[8388608]{0:T(1024)(128)(4,1)}), s8[4194304]{0:T(1024)(128)(4,1)S(1)}, s32[]{:S(2)}) async-start(s8[8388608]{0:T(1024)(128)(4,1)} %bitcast.60), calls=%async_computation.8 | async-start | bytes 8388608
  25.2 10.0 %copy-start.26 = (f32[392,4096]{1,0:T(8,128)}, f32[392,4096]{1,0:T(8,128)S(1)}, u32[]{:S(2)}) copy-start(f32[392,4096]{1,0:T(8,128)S(1)} %fusion.47) | copy-start | bytes 19267588
  25.2 10.0 %slice-start.1 = ((s8[8388608]{0:T(1024)(128)(4,1)}), s8[4194304]{0:T(1024)(128)(4,1)S(1)}, s32[]{:S(2)}) async-start(s8[8388608]{0:T(1024)(128)(4,1)} %bitcast.60), calls=%async_computation.9 | async-start | bytes 8388608
  35.2 4.8 copy-start.29
  42.3 3.1 copy-start.27
  44.5 3.6 copy-start.1
  45.8 2.4 copy-start.24
  50.9 241.0 %reduce-scatter.12.cloned.1.call-start = ((), (), s32[]{:S(2)}) async-start(), calls=%async_computation.5 | async-start | bytes 17825792
  79.1 393.4 %reduce-scatter.8.cloned.1.call-start = ((), (), s32[]{:S(2)}) async-start(), calls=%async_computation.3 | async-start | bytes 17825792 | tf_op jit(solution)/shard_map/reduce_scatter | solution.py:79
  90.3 408.3 %all-reduce.6.cloned.1.call-start = ((), (), s32[]{:S(2)}) async-start(), calls=%async_computation.6 | async-start | bytes 505856 | tf_op jit(solution)/shard_map/psum | solution.py:104
  93.1 198.8 %copy-start.7 = (f32[2,1024,196]{1,2,0:T(8,128)}, f32[2,1024,196]{1,2,0:T(8,128)S(1)}, u32[]{:S(2)}) copy-start(f32[2,1024,196]{1,2,0:T(8,128)S(1)} %get-tuple-element.64) | copy-start | bytes 4816900
  158.8 428.0 %all-reduce.8.cloned.1.call-start = ((), (), s32[]{:S(2)}) async-start(), calls=%async_computation.7 | async-start | bytes 6291456 | tf_op jit(solution)/shard_map/psum | solution.py:104
  295.2 177.4 %copy-start.2 = (f32[2,196,1024]{2,1,0:T(8,128)S(1)}, f32[2,196,1024]{2,1,0:T(8,128)}, u32[]{:S(2)}) copy-start(f32[2,196,1024]{2,1,0:T(8,128)} %copy-done.1) | copy-start | bytes 4816900
  586.8 3.3 copy-start.9
  586.8 4.2 copy-start.16
  586.8 4.8 copy-start.20
  586.8 5.4 copy-start.21
  586.8 6.0 copy-start.17
  (13 other events, 21.2 us)
Sparse Core Ops, SparseCore 0:
  51.1 60.3 reduce-scatter.9
  115.6 176.3 reduce-scatter.11
  296.1 176.3 reduce-scatter.7
  476.0 22.5 all-reduce.5
  500.8 85.9 all-reduce.7
